TPU v7x, 32 devices: a whole 2x2x4 slice. The times are simulated.
32 devices in a mesh: grp: 16 (over z, y, x), node: 2 (over core).
Axes of the slice: x: 2, y: 2, z: 4, core: 2. Of those that a mesh axis runs over, the one named last changes fastest.
Arguments:
- grad_out: bfloat16 [6144, 2048], P('grp', 'node'), may hold values from -12 to 12
- gate_prob: float32 [6144], P('grp'), may hold values from 0.05 to 1
- hidden: bfloat16 [6144, 7168], P('grp', 'node'), may hold values from -0.19921875 to 0.19921875
- w_down: bfloat16 [2048, 7168], P(None, 'node'), may hold values from -0.0625 to 0.0625
- slot_counts: int32 [16], P('grp'), may hold values from 0 to 384, as said below
Outputs:
- grad_hidden: bfloat16 [6144, 7168], P('grp', 'node')
- grad_weight: bfloat16 [2048, 7168], P('grp', 'node')
Inputs may be any that keep to these rules, and one draw needn't show every extreme that they name: `slot_counts`: each count is a multiple of 128; in every draw some group's count is 384.
All inputs are finite; a program needn't handle non-finite values.
Results may differ from a plain program's by a relative error of at most 0.0057.
Values may be sent and summed in bfloat16 or wider, within the bound.
A program may use at most 128 MiB of HBM per device.

v0:
```python
import jax
import jax.numpy as jnp
from jax import lax
from jax.sharding import PartitionSpec as P

TILE_ROWS = 128


def hidden_grads(features, w_down, tile_rows, first_tile, tile_count):
    buffer_rows = features.shape[0]
    zeros_out = jnp.zeros((buffer_rows, w_down.shape[1]), jnp.bfloat16)

    def hidden_one_tile(tile_index, result):
        tile_block = lax.dynamic_slice_in_dim(features, tile_index * tile_rows, tile_rows, 0)
        product = jnp.dot(tile_block, w_down, preferred_element_type=jnp.float32).astype(
            jnp.bfloat16
        )
        return lax.dynamic_update_slice_in_dim(result, product, tile_index * tile_rows, 0)

    return lax.fori_loop(first_tile, first_tile + tile_count, hidden_one_tile, zeros_out)


def weight_term(features, hidden_part, tile_rows, tile_count):

    def weight_one_tile(tile_index, running):
        slot_block = lax.dynamic_slice_in_dim(features, tile_index * tile_rows, tile_rows, 0)
        unit_block = lax.dynamic_slice_in_dim(hidden_part, tile_index * tile_rows, tile_rows, 0)
        return running + lax.dot_general(
            slot_block, unit_block, (((0,), (0,)), ((), ())), preferred_element_type=jnp.float32
        )

    start_sum = jnp.zeros((features.shape[1], hidden_part.shape[1]), jnp.float32)
    return lax.fori_loop(0, tile_count, weight_one_tile, start_sum)


def owner_rows(received):
    return jnp.sum(received.astype(jnp.float32), axis=0)


def body(grad_out, gate_prob, hidden, w_down, slot_counts):
    tile_rows = TILE_ROWS
    own_tiles = slot_counts[0] // tile_rows
    scaled = (gate_prob[:, None] * grad_out.astype(jnp.float32)).astype(jnp.bfloat16)
    gathered = lax.all_gather(scaled, "node", axis=1, tiled=True)
    grad_hidden = hidden_grads(gathered, w_down, tile_rows, 0, own_tiles)
    group_count = lax.axis_size("grp")
    model_rows = gathered.shape[1]
    rows_here = model_rows // group_count
    unit_count = hidden.shape[1]
    split_at = unit_count // 2 // 128 * 128
    bounds = [(0, split_at), (split_at, unit_count)]
    summed_parts = []
    for low_col, high_col in bounds:
        part_term = weight_term(gathered, hidden[:, low_col:high_col], tile_rows, own_tiles).astype(
            jnp.bfloat16
        )
        blocks = part_term.reshape(group_count, rows_here, high_col - low_col)
        received = lax.all_to_all(blocks, "grp", split_axis=0, concat_axis=0, tiled=True)
        summed_parts.append(owner_rows(received))
    summed = jnp.concatenate(summed_parts, axis=1)
    return (grad_hidden, summed.astype(jnp.bfloat16))


def solution(mesh):
    return jax.shard_map(
        body,
        mesh=mesh,
        in_specs=(P("grp", "node"), P("grp"), P("grp", "node"), P(None, "node"), P("grp")),
        out_specs=(P("grp", "node"), P("grp", "node")),
        check_vma=False,
    )
```

profile of v0, /device:TPU:28, one launch (start us, length us, event | category | flops | bytes accessed | tf_op | source)
XLA Modules:
  0.0 430.7 jit_solution(9123053713077568909)
XLA Ops:
  7.2 0.0 all-gather.2.cloned.1.call-start
  7.2 2.2 multiply_convert_fusion
  9.4 0.0 all-gather.2.cloned.1.call-update
  10.1 3.0 fusion.9
  13.1 8.0 %all-gather.2.cloned.1.call-done = bf16[384,2048]{1,0:T(8,128)(2,1)} async-done(((bf16[384,1024]{1,0:T(8,128)(2,1)}), bf16[384,2048]{1,0:T(8,128)(2,1)}) %all-gather.2.cloned.1.call-update) | async-done | bytes 1572880 | tf_op jit(solution)/shard_map/all_gather | solution.py:44
  21.1 0.0 copy-start
  21.1 6.1 %broadcast.5.clone.1 = f32[2048,1792]{1,0:T(8,128)} broadcast(f32[]{:T(128)} %constant.45.clone.1), dimensions={} | broadcast | bytes 14680068 | tf_op jit(solution)/shard_map/broadcast.1
  27.3 0.0 copy-done
  27.3 12.7 %while.31 = (s32[]{:T(128)}, f32[2048,1792]{1,0:T(8,128)}, s32[]{:T(128)}, bf16[384,2048]{1,0:T(8,128)(2,1)S(1)}, bf16[384,1792]{1,0:T(8,128)(2,1)}, /*index=5*/s32[]{:T(128)}, s32[]{:T(128)}, s32[]{:T(128)}, s32[]{:T(128)}) while((s32[]{:T(128)}, f32[2048,1792]{1,0:T(8,128)}, s32[]{:T(128)}, bf16[384,2048]{1,0:T(8,128)(2,1)S(1)}, ...), condition=%wide.region_3.4_spmd, body=%wide.region_2.3_spmd.sunk | while | flops 943194112 | bytes 30344332 | solution.py:33
  27.3 12.6 %convolution_add_fusion.4 = f32[2048,1792]{1,0:T(8,128)} fusion(f32[2048,1792]{1,0:T(8,128)} %get-tuple-element.281, bf16[384,2048]{1,0:T(8,128)(2,1)S(1)} %get-tuple-element.292, s32[]{:T(128)S(6)} %select_n.22, bf16[384,1792]{1,0:T(8,128)(2,1)} %get-tuple-element.293), kind=kOutput, calls=%fused_computation.4.clone.1 | convolution fusion | flops 943194112 | bytes 30344192 | tf_op jit(solution)/shard_map/while/body/dot_general | solution.py:28
  39.9 8.8 %convert_element_type.24 = bf16[2048,1792]{1,0:T(8,128)(2,1)} convert(f32[2048,1792]{1,0:T(8,128)} %get-tuple-element.87) | non-fusion elementwise | flops 3670016 | bytes 22020096 | tf_op jit(solution)/shard_map/convert_element_type | solution.py:54
  48.8 32.2 %all-to-all-start = ((bf16[16,128,1792]{2,1,0:T(8,128)(2,1)}), bf16[16,128,1792]{2,1,0:T(8,128)(2,1)}, u32[]{:S(2)}, u32[]{:S(2)}) async-start(bf16[16,128,1792]{2,1,0:T(8,128)(2,1)} %bitcast.11), calls=%async_computation | async-start | bytes 14680064 | tf_op jit(solution)/shard_map/all_to_all | solution.py:58
  81.0 6.1 %broadcast.5.clone = f32[2048,1792]{1,0:T(8,128)} broadcast(f32[]{:T(128)} %constant.45.clone.1), dimensions={} | broadcast | bytes 14680068 | tf_op jit(solution)/shard_map/broadcast.1
  87.1 12.5 %while.32 = (s32[]{:T(128)}, f32[2048,1792]{1,0:T(8,128)}, s32[]{:T(128)}, bf16[384,2048]{1,0:T(8,128)(2,1)S(1)}, bf16[384,1792]{1,0:T(8,128)(2,1)S(1)}, /*index=5*/s32[]{:T(128)}, s32[]{:T(128)}, s32[]{:T(128)}, s32[]{:T(128)}) while((s32[]{:T(128)}, f32[2048,1792]{1,0:T(8,128)}, s32[]{:T(128)}, bf16[384,2048]{1,0:T(8,128)(2,1)S(1)}, ...), condition=%wide.region_6.7_spmd, body=%wide.region_5.6_spmd.sunk | while | flops 943194112 | bytes 30344332 | solution.py:33
  87.1 12.5 %convolution_add_fusion.5 = f32[2048,1792]{1,0:T(8,128)} fusion(f32[2048,1792]{1,0:T(8,128)} %get-tuple-element.254, bf16[384,2048]{1,0:T(8,128)(2,1)S(1)} %get-tuple-element.265, s32[]{:T(128)S(6)} %select_n.23, bf16[384,1792]{1,0:T(8,128)(2,1)S(1)} %get-tuple-element.266), kind=kOutput, calls=%fused_computation.8.clone.1 | convolution fusion | flops 943194112 | bytes 30344192 | tf_op jit(solution)/shard_map/while/body/dot_general | solution.py:28
  99.6 8.8 %convert_element_type.26 = bf16[2048,1792]{1,0:T(8,128)(2,1)} convert(f32[2048,1792]{1,0:T(8,128)} %get-tuple-element.88) | non-fusion elementwise | flops 3670016 | bytes 22020096 | tf_op jit(solution)/shard_map/convert_element_type | solution.py:54
  108.4 139.7 %all-to-all-done = bf16[16,128,1792]{2,1,0:T(8,128)(2,1)} async-done(((bf16[16,128,1792]{2,1,0:T(8,128)(2,1)}), bf16[16,128,1792]{2,1,0:T(8,128)(2,1)}, u32[]{:S(2)}, u32[]{:S(2)}) %all-to-all-start) | async-done | bytes 7340064 | tf_op jit(solution)/shard_map/all_to_all | solution.py:58
  248.1 6.0 %all-to-all-start.1 = ((bf16[16,128,1792]{2,1,0:T(8,128)(2,1)}), bf16[16,128,1792]{2,1,0:T(8,128)(2,1)}, u32[]{:S(2)}, u32[]{:S(2)}) async-start(bf16[16,128,1792]{2,1,0:T(8,128)(2,1)} %bitcast.10), calls=%async_computation.1 | async-start | bytes 14680064 | tf_op jit(solution)/shard_map/all_to_all | solution.py:58
  254.1 1.7 broadcast_in_dim.4
  255.9 8.2 %while.30 = (s32[]{:T(128)}, bf16[384,3584]{1,0:T(8,128)(2,1)}, s32[]{:T(128)}, bf16[384,2048]{1,0:T(8,128)(2,1)S(1)}, bf16[2048,3584]{1,0:T(8,128)(2,1)}, /*index=5*/s32[]{:T(128)}, s32[]{:T(128)}, s32[]{:T(128)}, s32[]{:T(128)}) while((s32[]{:T(128)}, bf16[384,3584]{1,0:T(8,128)(2,1)}, s32[]{:T(128)}, bf16[384,2048]{1,0:T(8,128)(2,1)S(1)}, ...), condition=%wide.region_1.2_spmd, body=%wide.region_0.1_spmd.sunk | while | flops 1879506944 | bytes 16123019 | solution.py:20
  255.9 8.2 %fusion.20 = bf16[384,3584]{1,0:T(8,128)(2,1)} fusion(bf16[384,3584]{1,0:T(8,128)(2,1)} %get-tuple-element.227, s32[]{:T(128)S(6)} %select_n.21, bf16[2048,3584]{1,0:T(8,128)(2,1)} %get-tuple-element.239, bf16[384,2048]{1,0:T(8,128)(2,1)S(1)} %get-tuple-element.238), kind=kOutput, calls=%fused_computation.1.clone.1 | convolution fusion | flops 1879506944 | bytes 16122880 | tf_op jit(solution)/shard_map/while/body/dot_general | solution.py:15
  264.0 4.3 reduce
  268.3 150.3 %all-to-all-done.1 = bf16[16,128,1792]{2,1,0:T(8,128)(2,1)} async-done(((bf16[16,128,1792]{2,1,0:T(8,128)(2,1)}), bf16[16,128,1792]{2,1,0:T(8,128)(2,1)}, u32[]{:S(2)}, u32[]{:S(2)}) %all-to-all-start.1) | async-done | bytes 7340064 | tf_op jit(solution)/shard_map/all_to_all | solution.py:58
  418.6 4.3 reduce.1
  422.9 1.0 pad_maximum_fusion
Async XLA Ops:
  7.2 14.0 %all-gather.2.cloned.1.call-start = ((), (), s32[]{:S(2)}) async-start(), calls=%async_computation.2 | async-start | bytes 2359296 | tf_op jit(solution)/shard_map/all_gather | solution.py:44
  21.1 6.1 %copy-start = (bf16[384,2048]{1,0:T(8,128)(2,1)S(1)}, bf16[384,2048]{1,0:T(8,128)(2,1)}, u32[]{:S(2)}) copy-start(bf16[384,2048]{1,0:T(8,128)(2,1)} %all-gather.2.cloned.1.call-done) | copy-start | bytes 4718596
  48.8 199.4 %all-to-all-start = ((bf16[16,128,1792]{2,1,0:T(8,128)(2,1)}), bf16[16,128,1792]{2,1,0:T(8,128)(2,1)}, u32[]{:S(2)}, u32[]{:S(2)}) async-start(bf16[16,128,1792]{2,1,0:T(8,128)(2,1)} %bitcast.11), calls=%async_computation | async-start | bytes 14680064 | tf_op jit(solution)/shard_map/all_to_all | solution.py:58
  248.1 170.5 %all-to-all-start.1 = ((bf16[16,128,1792]{2,1,0:T(8,128)(2,1)}), bf16[16,128,1792]{2,1,0:T(8,128)(2,1)}, u32[]{:S(2)}, u32[]{:S(2)}) async-start(bf16[16,128,1792]{2,1,0:T(8,128)(2,1)} %bitcast.10), calls=%async_computation.1 | async-start | bytes 14680064 | tf_op jit(solution)/shard_map/all_to_all | solution.py:58
Sparse Core Ops, SparseCore 0:
  10.1 10.9 all-gather.1
where the time goes:
time: 431 us
  waiting for transfers between devices  298 us (69%)
  starting transfers between devices  38.3 us (9%)
  matrix products  33.3 us (8%)
  other arithmetic  29.4 us (7%)
  local copies, waits for them, and re-layouts  17 us (4%)
  between operations  14.7 us (3%)
    all_to_all x2, waiting for transfers between devices, body(): lax.all_to_all(blocks, 'grp', split_axis=0, concat_axis=0, tiled=True)  290 us
    all_to_all x2, starting transfers between devices, body(): lax.all_to_all(blocks, 'grp', split_axis=0, concat_axis=0, tiled=True)  38.2 us
    dot_general x2, matrix products, weight_one_tile(): lax.dot_general(slot_block, unit_block, (((0,), (0,)), ((), ())), preferr...  25.1 us
    convert_element_type x2, other arithmetic, body(): weight_term(gathered, hidden[:, low_col:high_col], tile_rows, own_tiles)  17.7 us
    another operation x2, local copies, waits for them, and re-layouts  12.3 us
  transfers between devices with their start and end apart: 3, of which 3 were waited for; matrix products, arithmetic and copies ran while one was open for 10% of the time, Pallas kernels for 0%

commit v1 on v0

v1 whole, which is shorter than its diff:
```python
import jax
import jax.numpy as jnp
from jax import lax
from jax.sharding import PartitionSpec as P


def body(grad_out, gate_prob, hidden, w_down, slot_counts):
    rows = grad_out.shape[0]
    live = lax.iota(jnp.int32, rows) < slot_counts[0]
    scaled = (gate_prob[:, None] * grad_out.astype(jnp.float32)).astype(jnp.bfloat16)
    scaled = jnp.where(live[:, None], scaled, jnp.zeros_like(scaled))
    gathered = lax.all_gather(scaled, "node", axis=1, tiled=True)
    term = lax.dot_general(
        gathered, hidden, (((0,), (0,)), ((), ())), preferred_element_type=jnp.float32
    ).astype(jnp.bfloat16)
    summed = lax.psum_scatter(term, "grp", scatter_dimension=0, tiled=True)
    grad_hidden = jnp.dot(gathered, w_down, preferred_element_type=jnp.float32).astype(jnp.bfloat16)
    return (grad_hidden, summed)


def solution(mesh):
    return jax.shard_map(
        body,
        mesh=mesh,
        in_specs=(P("grp", "node"), P("grp"), P("grp", "node"), P(None, "node"), P("grp")),
        out_specs=(P("grp", "node"), P("grp", "node")),
        check_vma=False,
    )
```

time: 431 us -> 352 us (0.82)
  the two profiles are of different devices: /device:TPU:28 before, /device:TPU:0 now
where the time goes in v1:
time: 352 us; the launch traced here: 348 us
  waiting for transfers between devices  308 us (88%)
  matrix products  23.1 us (7%)
  between operations  14.8 us (4%)
    reduce_scatter x1, waiting for transfers between devices, body(): summed = lax.psum_scatter(term, 'grp', scatter_dimension=0, tiled=True)  295 us
    all_gather x1, waiting for transfers between devices, body(): gathered = lax.all_gather(scaled, 'node', axis=1, tiled=True)  12.6 us
    dot_general x1, matrix products, body(): lax.dot_general(gathered, hidden, (((0,), (0,)), ((), ())), preferred_ele...  12.5 us
    dot_general x1, matrix products, body(): jnp.dot(gathered, w_down, preferred_element_type=jnp.float32)  10.6 us
  transfers between devices with their start and end apart: 2, of which 2 were waited for; matrix products, arithmetic and copies ran while one was open for 3% of the time, Pallas kernels for 0%

profile of v1, /device:TPU:0, one launch (start us, length us, event | category | flops | bytes accessed | tf_op | source)
XLA Modules:
  0.0 347.9 jit_solution(11390456932358173893)
XLA Ops:
  7.2 0.0 copy-start
  7.2 0.0 all-gather.2.cloned.1.call-start
  8.0 2.3 fusion
  10.3 0.0 all-gather.2.cloned.1.call-update
  10.3 0.0 reduce-scatter.2.cloned.1.call-start
  10.4 12.6 %all-gather.2.cloned.1.call-done = bf16[384,2048]{1,0:T(8,128)(2,1)} async-done(((bf16[384,1024]{1,0:T(8,128)(2,1)}), bf16[384,2048]{1,0:T(8,128)(2,1)}) %all-gather.2.cloned.1.call-update) | async-done | bytes 1572880 | tf_op jit(solution)/shard_map/all_gather | solution.py:12
  23.0 0.0 copy-done
  23.0 12.5 %convolution_convert_fusion = bf16[2048,3584]{1,0:T(8,128)(2,1)} fusion(bf16[384,2048]{1,0:T(8,128)(2,1)} %all-gather.2.cloned.1.call-done, bf16[384,3584]{1,0:T(8,128)(2,1)S(1)} %copy-done), kind=kOutput, calls=%fused_computation | convolution fusion | flops 5644484608 | bytes 19005440 | tf_op jit(solution)/shard_map/dot_general | solution.py:13
  35.5 0.0 reduce-scatter.2.cloned.1.call-update
  35.5 10.6 %convolution_convert_fusion.1 = bf16[384,3584]{1,0:T(8,128)(2,1)} fusion(bf16[384,2048]{1,0:T(8,128)(2,1)} %all-gather.2.cloned.1.call-done, bf16[2048,3584]{1,0:T(8,128)(2,1)} %param.8), kind=kOutput, calls=%fused_computation.1 | convolution fusion | flops 5638520832 | bytes 19005440 | tf_op jit(solution)/shard_map/dot_general | solution.py:17
  46.2 294.9 %reduce-scatter.2.cloned.1.call-done = bf16[128,3584]{1,0:T(8,128)(2,1)} async-done(((bf16[2048,3584]{1,0:T(8,128)(2,1)}), bf16[128,3584]{1,0:T(8,128)(2,1)}) %reduce-scatter.2.cloned.1.call-update) | async-done | bytes 917520 | tf_op jit(solution)/shard_map/reduce_scatter | solution.py:16
  (1 shorter events, 0.0 us)
Async XLA Ops:
  7.2 15.8 %copy-start = (bf16[384,3584]{1,0:T(8,128)(2,1)S(1)}, bf16[384,3584]{1,0:T(8,128)(2,1)}, u32[]{:S(2)}) copy-start(bf16[384,3584]{1,0:T(8,128)(2,1)} %param.7) | copy-start | bytes 8257540
  7.2 15.8 %all-gather.2.cloned.1.call-start = ((), (), s32[]{:S(2)}) async-start(), calls=%async_computation.1 | async-start | bytes 2359296 | tf_op jit(solution)/shard_map/all_gather | solution.py:12
  10.3 330.8 %reduce-scatter.2.cloned.1.call-start = ((), (), s32[]{:S(2)}) async-start(), calls=%async_computation.2 | async-start | bytes 15597568 | tf_op jit(solution)/shard_map/reduce_scatter | solution.py:16
Sparse Core Ops, SparseCore 0:
  10.4 12.5 all-gather.1
  35.7 305.3 reduce-scatter.1

commit v2 on v1

v2 whole, which is shorter than its diff:
```python
import functools

import jax
import jax.numpy as jnp
from jax import lax
from jax.experimental import pallas as pl
from jax.experimental.pallas import tpu as pltpu
from jax.sharding import PartitionSpec as P

MESH = pl.DeviceIdType.MESH
LANES = 128
AHEAD = 2
F32, BF16 = jnp.float32, jnp.bfloat16


def added(a, b):
    return (a.astype(F32) + b.astype(F32)).astype(BF16)


def kernel(
    dims, s_ref, st_ref, hid_ref, w_ref, gh_ref, gw_ref,
    g, gt, acc, rx1, rx2, up, dn, wbuf,
    gsend, grecv, send1, recv1, send2, recv2, usend, urecv, dsend, drecv, wsem,
):
    nodes, depth, chunks = dims
    node = lax.axis_index("node")
    me = lax.axis_index("grp")
    mx, my, mz = me % 2, (me // 2) % 2, me // 4
    px, py = 1 - mx, 1 - my
    half = s_ref.shape[1]
    wide = 2 * LANES
    rows = acc.shape[5]
    last = depth - 1
    not_first, not_last = mz > 0, mz < last

    def grp_at(z, y, x):
        return {"grp": (z * 2 + y) * 2 + x}

    to_x, to_y = grp_at(mz, my, px), grp_at(mz, py, mx)
    to_up, to_down = {"grp": me + 4}, {"grp": me - 4}

    barrier = pltpu.get_barrier_semaphore()

    def greet(target):
        pl.semaphore_signal(barrier, inc=1, device_id=target, device_id_type=MESH)

    greet(to_x)
    greet(to_y)
    for off in range(1, nodes):
        greet({"node": (node + off) % nodes})

    @pl.when(not_first)
    def _():
        greet(to_down)

    @pl.when(not_last)
    def _():
        greet(to_up)

    def w_copy(c, slot):
        cols = pl.ds(pl.multiple_of(c * wide, wide), wide)
        return pltpu.make_async_copy(w_ref.at[:, cols], wbuf.at[slot], wsem.at[slot])

    w_copy(0, 0).start()
    pl.semaphore_wait(
        barrier, 1 + nodes + not_first.astype(jnp.int32) + not_last.astype(jnp.int32)
    )

    def remote(src, dst, ssem, rsem, target):
        return pltpu.make_async_remote_copy(
            src_ref=src, dst_ref=dst, send_sem=ssem, recv_sem=rsem,
            device_id=target, device_id_type=MESH,
        )

    def own_rows(i):
        return pl.ds(pl.multiple_of(i * half, half), half)

    def exchange(off):
        target = {"node": (node + off) % nodes}
        return (
            remote(st_ref, gt.at[own_rows(node)], gsend.at[0, off], grecv.at[0, off], target),
            remote(s_ref, g.at[node], gsend.at[1, off], grecv.at[1, off], target),
        )

    for off in range(1, nodes):
        for copy in exchange(off):
            copy.start()
    gt[own_rows(node), :] = st_ref[...]
    g[node] = s_ref[...]
    for off in range(1, nodes):
        for copy in exchange(off):
            copy.wait()

    def first(kind, c):
        if kind == 0:
            src, target = acc.at[0, c, :, :, px], to_x
        else:
            src, target = acc.at[1, c, :, py], to_y
        return remote(src, rx1.at[kind, c], send1.at[kind, c], recv1.at[kind, c], target)

    def second(kind, c):
        if kind == 0:
            src, target = acc.at[0, c, :, py, mx], to_y
        else:
            src, target = acc.at[1, c, :, my, px], to_x
        return remote(src, rx2.at[kind, c], send2.at[kind, c], recv2.at[kind, c], target)

    def line(c, d, rising):
        src = acc.at[:, c, d, my, mx]
        if rising:
            return remote(src, up.at[c, d], usend.at[c, d], urecv.at[c, d], to_up)
        return remote(src, dn.at[c, d], dsend.at[c, d], drecv.at[c, d], to_down)


    def make_term(c):
        cols = pl.ds(pl.multiple_of(c * wide, wide), wide)
        units = hid_ref[:, cols]

        def one(z, carry):
            part = gt[pl.ds(pl.multiple_of(z * 4 * rows, 4 * rows), 4 * rows), :]
            product = jnp.dot(part, units, preferred_element_type=F32).astype(BF16)
            product = product.reshape(2, 2, rows, wide)
            acc[0, c, z] = product[..., :LANES]
            acc[1, c, z] = product[..., LANES:]
            return carry

        lax.fori_loop(0, depth, one, 0)

    def make_hidden(c):
        slot = c % 2
        w_copy(c, slot).wait()

        @pl.when(c + 1 < chunks)
        def _():
            w_copy(c + 1, 1 - slot).start()

        total = jnp.dot(g[0], wbuf[slot, :half, :], preferred_element_type=F32)
        for i in range(1, nodes):
            total += jnp.dot(
                g[i], wbuf[slot, i * half : (i + 1) * half, :], preferred_element_type=F32
            )
        gh_ref[:, pl.ds(pl.multiple_of(c * wide, wide), wide)] = total.astype(BF16)

    def within(c, run):
        @pl.when((c >= 0) & (c < chunks))
        def _():
            run(c)

    def step_make(c):
        make_term(c)
        first(0, c).start()
        first(1, c).start()
        make_hidden(c)

    def step_second(c):
        first(0, c).wait_recv()
        acc[0, c, :, :, mx] = added(acc[0, c, :, :, mx], rx1[0, c])
        second(0, c).start()
        first(1, c).wait_recv()
        acc[1, c, :, my] = added(acc[1, c, :, my], rx1[1, c])
        second(1, c).start()

    def step_column(c):
        for kind in range(2):
            second(kind, c).wait_recv()
            acc[kind, c, :, my, mx] = added(acc[kind, c, :, my, mx], rx2[kind, c])

        @pl.when(mz == 0)
        def _():
            for d in range(last, 0, -1):
                line(c, d, True).start()

        @pl.when(mz == last)
        def _():
            for d in range(last):
                line(c, d, False).start()

    def step_rise(c):
        for d in range(last, 0, -1):
            @pl.when(d >= mz)
            def _():
                line(c, d, True).wait_recv()

            @pl.when(d > mz)
            def _():
                acc[:, c, d, my, mx] = added(acc[:, c, d, my, mx], up[c, d])
                line(c, d, True).start()

    def step_fall(c):
        for d in range(last):
            @pl.when(d <= mz)
            def _():
                line(c, d, False).wait_recv()

            @pl.when(d < mz)
            def _():
                acc[:, c, d, my, mx] = added(acc[:, c, d, my, mx], dn[c, d])
                line(c, d, False).start()

    def step_final(c):
        def put(total):
            for kind in range(2):
                cols = pl.ds(pl.multiple_of(c * wide + kind * LANES, LANES), LANES)
                gw_ref[:, cols] = total[kind].astype(BF16)

        @pl.when(mz == 0)
        def _():
            put(acc[:, c, mz, my, mx].astype(F32) + dn[c, mz].astype(F32))

        @pl.when(mz == last)
        def _():
            put(acc[:, c, mz, my, mx].astype(F32) + up[c, mz].astype(F32))

        @pl.when(not_first & not_last)
        def _():
            put(
                acc[:, c, mz, my, mx].astype(F32)
                + up[c, mz].astype(F32)
                + dn[c, mz].astype(F32)
            )

    def step(t, carry):
        within(t, step_make)
        within(t - AHEAD, step_second)
        column = t - AHEAD - 1
        within(column, step_column)

        @pl.when(not_first)
        def _():
            within(column - mz, step_rise)

        @pl.when(not_last)
        def _():
            within(column - (last - mz), step_fall)

        within(column - last, step_final)
        return carry

    lax.fori_loop(0, chunks + AHEAD + 1 + last, step, 0)

    def drain(c, carry):
        for kind in range(2):
            first(kind, c).wait_send()
            second(kind, c).wait_send()
        for d in range(depth):
            @pl.when(d > mz)
            def _():
                line(c, d, True).wait_send()

            @pl.when(d < mz)
            def _():
                line(c, d, False).wait_send()
        return carry

    lax.fori_loop(0, chunks, drain, 0)


def body(grad_out, gate_prob, hidden, w_down, slot_counts):
    slots, half = grad_out.shape
    nodes, groups = lax.axis_size("node"), lax.axis_size("grp")
    depth = groups // 4
    model = w_down.shape[0]
    rows = model // groups
    units = hidden.shape[1]
    wide = 2 * LANES
    chunks = -(-units // wide)
    extra = chunks * wide - units
    live = lax.iota(jnp.int32, slots) < slot_counts[0]
    scaled = (gate_prob[:, None] * grad_out.astype(F32)).astype(BF16)
    scaled = jnp.where(live[:, None], scaled, jnp.zeros_like(scaled))
    if extra:
        hidden = jnp.pad(hidden, ((0, 0), (0, extra)))
        w_down = jnp.pad(w_down, ((0, 0), (0, extra)))
    dma = pltpu.SemaphoreType.DMA
    vmem = pl.BlockSpec(memory_space=pltpu.VMEM)
    grad_hidden, grad_weight = pl.pallas_call(
        functools.partial(kernel, (nodes, depth, chunks)),
        out_shape=(
            jax.ShapeDtypeStruct((slots, chunks * wide), BF16),
            jax.ShapeDtypeStruct((rows, chunks * wide), BF16),
        ),
        in_specs=[vmem, vmem, vmem, pl.BlockSpec(memory_space=pl.ANY)],
        out_specs=(vmem, vmem),
        scratch_shapes=[
            pltpu.VMEM((nodes, slots, half), BF16),
            pltpu.VMEM((model, slots), BF16),
            pltpu.VMEM((2, chunks, depth, 2, 2, rows, LANES), BF16),
            pltpu.VMEM((2, chunks, depth, 2, rows, LANES), BF16),
            pltpu.VMEM((2, chunks, depth, rows, LANES), BF16),
            pltpu.VMEM((chunks, depth, 2, rows, LANES), BF16),
            pltpu.VMEM((chunks, depth, 2, rows, LANES), BF16),
            pltpu.VMEM((2, model, wide), BF16),
            dma((2, nodes)),
            dma((2, nodes)),
            dma((2, chunks)),
            dma((2, chunks)),
            dma((2, chunks)),
            dma((2, chunks)),
            dma((chunks, depth)),
            dma((chunks, depth)),
            dma((chunks, depth)),
            dma((chunks, depth)),
            dma((2,)),
        ],
        compiler_params=pltpu.CompilerParams(
            collective_id=0, has_side_effects=True, vmem_limit_bytes=60 * 1024 * 1024
        ),
    )(scaled, scaled.T, hidden, w_down)
    return grad_hidden[:, :units], grad_weight[:, :units]


def solution(mesh):
    return jax.shard_map(
        body,
        mesh=mesh,
        in_specs=(P("grp", "node"), P("grp"), P("grp", "node"), P(None, "node"), P("grp")),
        out_specs=(P("grp", "node"), P("grp", "node")),
        check_vma=False,
    )
```

time: 352 us -> 161 us (0.46); the launches traced: 348 us -> 161 us
  waiting for transfers between devices: 308 us -> 0 us
  Pallas kernels: 0 us -> 151 us
  matrix products: 23.1 us -> 0 us
  between operations: 14.8 us -> 1.34 us
  local copies, waits for them, and re-layouts: 0.01 us -> 7.16 us
    reduce_scatter x1 -> x0, waiting for transfers between devices: 295 us -> none  [body(): summed = lax.psum_scatter(term, 'grp', scatter_dimension=0, tiled=True)]
    pallas_call x0 -> x1, Pallas kernels: none -> 151 us  [body(): pl.pallas_call(functools.partial(kernel, (nodes, depth, chunks)), out_sha...]
    dot_general x2 -> x0, matrix products: 23.1 us -> none  [the longest x1 12.5 us: body(): lax.dot_general(gathered, hidden, (((0,), (0,)), ((), ())), preferred_ele...]
    all_gather x1 -> x0, waiting for transfers between devices: 12.6 us -> none  [body(): gathered = lax.all_gather(scaled, 'node', axis=1, tiled=True)]
    unnamed x2 -> x7, local copies, waits for them, and re-layouts: 0.01 us -> 5.99 us
  transfers between devices with their start and end apart: 2 -> 0, of which waited for: 2 -> 0; matrix products, arithmetic and copies ran while one was open for 3% -> 0% of each run, Pallas kernels for 0% -> 0%
where the time goes in v2:
time: 161 us
  Pallas kernels  151 us (94%)
  local copies, waits for them, and re-layouts  7.16 us (4%)
    pallas_call x1, Pallas kernels, body(): pl.pallas_call(functools.partial(kernel, (nodes, depth, chunks)), out_sha...  151 us
    unnamed x7, local copies, waits for them, and re-layouts  5.99 us

profile of v2, /device:TPU:0, one launch (start us, length us, event | category | flops | bytes accessed | tf_op | source)
XLA Modules:
  0.0 160.6 jit_solution(9958593487963652784)
XLA Ops:
  0.6 0.0 copy-start.1
  1.3 1.5 copy.7
  2.8 0.0 copy-done.1
  2.8 1.1 fusion.1.st_ref
  3.9 0.2 fusion
  4.1 1.2 copy.8.s_ref
  5.3 150.8 %shard_map.68 = (bf16[384,3584]{1,0:T(8,128)(2,1)}, bf16[128,3584]{1,0:T(8,128)(2,1)}) custom-call(bf16[384,1024]{1,0:T(8,128)(2,1)} %copy.8.s_ref, bf16[1024,384]{1,0:T(8,128)(2,1)} %fusion.1.st_ref, bf16[384,3584]{1,0:T(8,128)(2,1)} %hid_ref.1, bf16[2048,3584]{1,0:T(8,128)(2,1)} %w_ref.1), custom_call_target="tpu_custom_call" | custom-call | tf_op jit(solution)/shard_map/pallas_call | solution.py:276
  156.1 0.0 copy-start
  156.1 3.6 %copy.12 = bf16[384,3584]{1,0:T(8,128)(2,1)} copy(bf16[384,3584]{1,0:T(8,128)(2,1)} %get-tuple-element.4) | data formatting | bytes 5505024
  159.6 0.0 copy-done
  159.6 0.9 copy.13
  (1 shorter events, 0.0 us)
Async XLA Ops:
  0.6 2.2 %copy-start.1 = (f32[384]{0:T(512)S(1)}, f32[384]{0:T(512)}, u32[]{:S(2)}) copy-start(f32[384]{0:T(512)} %param.6) | copy-start | bytes 4612
  156.1 3.6 %copy-start = (bf16[128,3584]{1,0:T(8,128)(2,1)S(1)}, bf16[128,3584]{1,0:T(8,128)(2,1)}, u32[]{:S(2)}) copy-start(bf16[128,3584]{1,0:T(8,128)(2,1)} %get-tuple-element.5) | copy-start | bytes 2752516

commit v3 on v2

--- a/solution.py
+++ b/solution.py
@@ -10,6 +10,7 @@
 MESH = pl.DeviceIdType.MESH
 LANES = 128
 AHEAD = 2
+HOP = 1
 F32, BF16 = jnp.float32, jnp.bfloat16
 
 
@@ -18,11 +19,13 @@
 
 
 def kernel(
-    dims, s_ref, st_ref, hid_ref, w_ref, gh_ref, gw_ref,
-    g, gt, acc, rx1, rx2, up, dn, wbuf,
+    dims, s_ref, st_ref, hid_any, w_ref, gh_ref, gw_ref,
+    g, gt, acc, rx1, rx2, up, dn, wbuf, hid_ref, zacc, zup, zdn, za, zb,
     gsend, grecv, send1, recv1, send2, recv2, usend, urecv, dsend, drecv, wsem,
+    zusend, zurecv, zdsend, zdrecv, zsend1, zrecv1, zsend2, zrecv2, hsem,
 ):
-    nodes, depth, chunks = dims
+    nodes, depth, chunks, zchunks = dims
+    total_chunks = chunks + zchunks
     node = lax.axis_index("node")
     me = lax.axis_index("grp")
     mx, my, mz = me % 2, (me // 2) % 2, me // 4
@@ -61,6 +64,8 @@
         cols = pl.ds(pl.multiple_of(c * wide, wide), wide)
         return pltpu.make_async_copy(w_ref.at[:, cols], wbuf.at[slot], wsem.at[slot])
 
+    fetch = pltpu.make_async_copy(hid_any, hid_ref, hsem)
+    fetch.start()
     w_copy(0, 0).start()
     pl.semaphore_wait(
         barrier, 1 + nodes + not_first.astype(jnp.int32) + not_last.astype(jnp.int32)
@@ -90,6 +95,7 @@
     for off in range(1, nodes):
         for copy in exchange(off):
             copy.wait()
+    fetch.wait()
 
     def first(kind, c):
         if kind == 0:
@@ -112,16 +118,16 @@
         return remote(src, dn.at[c, d], dsend.at[c, d], drecv.at[c, d], to_down)
 
 
-    def make_term(c):
-        cols = pl.ds(pl.multiple_of(c * wide, wide), wide)
+    def make_term(into, c, column):
+        cols = pl.ds(pl.multiple_of(column * wide, wide), wide)
         units = hid_ref[:, cols]
 
         def one(z, carry):
             part = gt[pl.ds(pl.multiple_of(z * 4 * rows, 4 * rows), 4 * rows), :]
             product = jnp.dot(part, units, preferred_element_type=F32).astype(BF16)
             product = product.reshape(2, 2, rows, wide)
-            acc[0, c, z] = product[..., :LANES]
-            acc[1, c, z] = product[..., LANES:]
+            into[0, c, z] = product[..., :LANES]
+            into[1, c, z] = product[..., LANES:]
             return carry
 
         lax.fori_loop(0, depth, one, 0)
@@ -130,7 +136,7 @@
         slot = c % 2
         w_copy(c, slot).wait()
 
-        @pl.when(c + 1 < chunks)
+        @pl.when(c + 1 < total_chunks)
         def _():
             w_copy(c + 1, 1 - slot).start()
 
@@ -141,16 +147,15 @@
             )
         gh_ref[:, pl.ds(pl.multiple_of(c * wide, wide), wide)] = total.astype(BF16)
 
-    def within(c, run):
-        @pl.when((c >= 0) & (c < chunks))
+    def within(c, run, count=chunks):
+        @pl.when((c >= 0) & (c < count))
         def _():
             run(c)
 
     def step_make(c):
-        make_term(c)
+        make_term(acc, c, c)
         first(0, c).start()
         first(1, c).start()
-        make_hidden(c)
 
     def step_second(c):
         first(0, c).wait_recv()
@@ -219,24 +224,122 @@
                 + dn[c, mz].astype(F32)
             )
 
+    def zline(q, d, rising):
+        src = zacc.at[:, q, d]
+        if rising:
+            return remote(src, zup.at[q, d], zusend.at[q, d], zurecv.at[q, d], to_up)
+        return remote(src, zdn.at[q, d], zdsend.at[q, d], zdrecv.at[q, d], to_down)
+
+    def zfirst(kind, q):
+        if kind == 0:
+            src, target = zacc.at[0, q, mz, :, px], to_x
+        else:
+            src, target = zacc.at[1, q, mz, py], to_y
+        return remote(src, za.at[kind, q], zsend1.at[kind, q], zrecv1.at[kind, q], target)
+
+    def zsecond(kind, q):
+        if kind == 0:
+            src, target = zacc.at[0, q, mz, py, mx], to_y
+        else:
+            src, target = zacc.at[1, q, mz, my, px], to_x
+        return remote(src, zb.at[kind, q], zsend2.at[kind, q], zrecv2.at[kind, q], target)
+
+    def zmake(t):
+        @pl.when(t % last == 0)
+        def _():
+            make_term(zacc, t // last, chunks + t // last)
+
+    def zrise(m):
+        q, d = m // last, last - m % last
+
+        @pl.when(not_first & (d >= mz))
+        def _():
+            zline(q, d, True).wait_recv()
+            zacc[:, q, d] = added(zacc[:, q, d], zup[q, d])
+
+        @pl.when(d > mz)
+        def _():
+            zline(q, d, True).start()
+
+    def zfall(m):
+        q, d = m // last, m % last
+
+        @pl.when(not_last & (d <= mz))
+        def _():
+            zline(q, d, False).wait_recv()
+            zacc[:, q, d] = added(zacc[:, q, d], zdn[q, d])
+
+        @pl.when(d < mz)
+        def _():
+            zline(q, d, False).start()
+
+    def every_last(m, run):
+        @pl.when((m >= 0) & (m % last == 0) & (m < zchunks * last))
+        def _():
+            run(m // last)
+
+    def zstep_first(q):
+        zfirst(0, q).start()
+        zfirst(1, q).start()
+
+    def zstep_second(q):
+        zfirst(0, q).wait_recv()
+        zacc[0, q, mz, :, mx] = added(zacc[0, q, mz, :, mx], za[0, q])
+        zsecond(0, q).start()
+        zfirst(1, q).wait_recv()
+        zacc[1, q, mz, my] = added(zacc[1, q, mz, my], za[1, q])
+        zsecond(1, q).start()
+
+    def zstep_final(q):
+        for kind in range(2):
+            zsecond(kind, q).wait_recv()
+            cols = pl.ds(
+                pl.multiple_of((chunks + q) * wide + kind * LANES, LANES), LANES
+            )
+            gw_ref[:, cols] = added(zacc[kind, q, mz, my, mx], zb[kind, q])
+
     def step(t, carry):
         within(t, step_make)
+        within(t, zmake, zchunks * last)
+        @pl.when(mz == 0)
+        def _():
+            within(t, zrise, zchunks * last)
+
+        @pl.when(mz == last)
+        def _():
+            within(t, zfall, zchunks * last)
+
+        within(t, make_hidden, total_chunks)
         within(t - AHEAD, step_second)
+
+        @pl.when(not_first)
+        def _():
+            within(t - HOP * mz, zrise, zchunks * last)
+
+        @pl.when(not_last)
+        def _():
+            within(t - HOP * (last - mz), zfall, zchunks * last)
+
+        done = t - HOP * last
+        every_last(done, zstep_first)
+        every_last(done - 1, zstep_second)
+        every_last(done - 2, zstep_final)
         column = t - AHEAD - 1
         within(column, step_column)
 
         @pl.when(not_first)
         def _():
-            within(column - mz, step_rise)
+            within(column - HOP * mz, step_rise)
 
         @pl.when(not_last)
         def _():
-            within(column - (last - mz), step_fall)
-
-        within(column - last, step_final)
+            within(column - HOP * (last - mz), step_fall)
+
+        within(column - HOP * last, step_final)
         return carry
 
-    lax.fori_loop(0, chunks + AHEAD + 1 + last, step, 0)
+    steps = max(chunks + AHEAD + 1 + HOP * last, (zchunks - 1 + HOP) * last + 3, total_chunks)
+    lax.fori_loop(0, steps, step, 0)
 
     def drain(c, carry):
         for kind in range(2):
@@ -253,6 +356,22 @@
         return carry
 
     lax.fori_loop(0, chunks, drain, 0)
+
+    def zdrain(q, carry):
+        for kind in range(2):
+            zfirst(kind, q).wait_send()
+            zsecond(kind, q).wait_send()
+        for d in range(depth):
+            @pl.when(d > mz)
+            def _():
+                zline(q, d, True).wait_send()
+
+            @pl.when(d < mz)
+            def _():
+                zline(q, d, False).wait_send()
+        return carry
+
+    lax.fori_loop(0, zchunks, zdrain, 0)
 
 
 def body(grad_out, gate_prob, hidden, w_down, slot_counts):
@@ -263,8 +382,10 @@
     rows = model // groups
     units = hidden.shape[1]
     wide = 2 * LANES
-    chunks = -(-units // wide)
-    extra = chunks * wide - units
+    total_chunks = -(-units // wide)
+    zchunks = max(1, round(total_chunks * 3 / 14))
+    chunks = total_chunks - zchunks
+    extra = total_chunks * wide - units
     live = lax.iota(jnp.int32, slots) < slot_counts[0]
     scaled = (gate_prob[:, None] * grad_out.astype(F32)).astype(BF16)
     scaled = jnp.where(live[:, None], scaled, jnp.zeros_like(scaled))
@@ -274,12 +395,12 @@
     dma = pltpu.SemaphoreType.DMA
     vmem = pl.BlockSpec(memory_space=pltpu.VMEM)
     grad_hidden, grad_weight = pl.pallas_call(
-        functools.partial(kernel, (nodes, depth, chunks)),
+        functools.partial(kernel, (nodes, depth, chunks, zchunks)),
         out_shape=(
-            jax.ShapeDtypeStruct((slots, chunks * wide), BF16),
-            jax.ShapeDtypeStruct((rows, chunks * wide), BF16),
+            jax.ShapeDtypeStruct((slots, total_chunks * wide), BF16),
+            jax.ShapeDtypeStruct((rows, total_chunks * wide), BF16),
         ),
-        in_specs=[vmem, vmem, vmem, pl.BlockSpec(memory_space=pl.ANY)],
+        in_specs=[vmem, vmem] + [pl.BlockSpec(memory_space=pl.ANY)] * 2,
         out_specs=(vmem, vmem),
         scratch_shapes=[
             pltpu.VMEM((nodes, slots, half), BF16),
@@ -290,6 +411,12 @@
             pltpu.VMEM((chunks, depth, 2, rows, LANES), BF16),
             pltpu.VMEM((chunks, depth, 2, rows, LANES), BF16),
             pltpu.VMEM((2, model, wide), BF16),
+            pltpu.VMEM((slots, total_chunks * wide), BF16),
+            pltpu.VMEM((2, zchunks, depth, 2, 2, rows, LANES), BF16),
+            pltpu.VMEM((zchunks, depth, 2, 2, 2, rows, LANES), BF16),
+            pltpu.VMEM((zchunks, depth, 2, 2, 2, rows, LANES), BF16),
+            pltpu.VMEM((2, zchunks, 2, rows, LANES), BF16),
+            pltpu.VMEM((2, zchunks, rows, LANES), BF16),
             dma((2, nodes)),
             dma((2, nodes)),
             dma((2, chunks)),
@@ -301,6 +428,15 @@
             dma((chunks, depth)),
             dma((chunks, depth)),
             dma((2,)),
+            dma((zchunks, depth)),
+            dma((zchunks, depth)),
+            dma((zchunks, depth)),
+            dma((zchunks, depth)),
+            dma((2, zchunks)),
+            dma((2, zchunks)),
+            dma((2, zchunks)),
+            dma((2, zchunks)),
+            dma(()),
         ],
         compiler_params=pltpu.CompilerParams(
             collective_id=0, has_side_effects=True, vmem_limit_bytes=60 * 1024 * 1024

time: 161 us -> 141 us (0.88)
  Pallas kernels: 151 us -> 131 us
    pallas_call x1, Pallas kernels: 151 us -> 131 us  [body(): pl.pallas_call(functools.partial(kernel, (nodes, depth, chunks, zchunks))...]
where the time goes in v3:
time: 141 us
  Pallas kernels  131 us (93%)
  local copies, waits for them, and re-layouts  7.16 us (5%)
    pallas_call x1, Pallas kernels, body(): pl.pallas_call(functools.partial(kernel, (nodes, depth, chunks, zchunks))...  131 us
    unnamed x7, local copies, waits for them, and re-layouts  5.99 us

profile of v3, /device:TPU:0, one launch (start us, length us, event | category | flops | bytes accessed | tf_op | source)
XLA Modules:
  0.0 140.7 jit_solution(7839871582692187882)
XLA Ops:
  0.6 0.0 copy-start.1
  1.3 1.5 %copy.7 = bf16[384,1024]{0,1:T(8,128)(2,1)S(1)} copy(bf16[384,1024]{1,0:T(8,128)(2,1)} %param.5) | data formatting | bytes 1572864 | tf_op args[0]
  2.8 0.0 copy-done.1
  2.8 1.1 fusion.1.st_ref
  3.9 0.2 fusion
  4.1 1.2 copy.8.s_ref
  5.3 131.0 %shard_map.68 = (bf16[384,3584]{1,0:T(8,128)(2,1)}, bf16[128,3584]{1,0:T(8,128)(2,1)}) custom-call(bf16[384,1024]{1,0:T(8,128)(2,1)} %copy.8.s_ref, bf16[1024,384]{1,0:T(8,128)(2,1)} %fusion.1.st_ref, bf16[384,3584]{1,0:T(8,128)(2,1)} %hid_any.1, bf16[2048,3584]{1,0:T(8,128)(2,1)} %w_ref.1), custom_call_target="tpu_custom_call" | custom-call | tf_op jit(solution)/shard_map/pallas_call | solution.py:397
  136.2 0.0 copy-start
  136.2 3.6 %copy.12 = bf16[384,3584]{1,0:T(8,128)(2,1)} copy(bf16[384,3584]{1,0:T(8,128)(2,1)} %get-tuple-element.4) | data formatting | bytes 5505024
  139.8 0.0 copy-done
  139.8 0.9 copy.13
  (1 shorter events, 0.0 us)
Async XLA Ops:
  0.6 2.2 %copy-start.1 = (f32[384]{0:T(512)S(1)}, f32[384]{0:T(512)}, u32[]{:S(2)}) copy-start(f32[384]{0:T(512)} %param.6) | copy-start | bytes 4612
  136.2 3.6 %copy-start = (bf16[128,3584]{1,0:T(8,128)(2,1)S(1)}, bf16[128,3584]{1,0:T(8,128)(2,1)}, u32[]{:S(2)}) copy-start(bf16[128,3584]{1,0:T(8,128)(2,1)} %get-tuple-element.5) | copy-start | bytes 2752516

commit v4 on v3

--- a/solution.py
+++ b/solution.py
@@ -9,8 +9,8 @@
 
 MESH = pl.DeviceIdType.MESH
 LANES = 128
-AHEAD = 2
-HOP = 1
+AHEAD = 1
+HOP = 2
 F32, BF16 = jnp.float32, jnp.bfloat16
 
 
@@ -19,8 +19,8 @@
 
 
 def kernel(
-    dims, s_ref, st_ref, hid_any, w_ref, gh_ref, gw_ref,
-    g, gt, acc, rx1, rx2, up, dn, wbuf, hid_ref, zacc, zup, zdn, za, zb,
+    dims, s_ref, hid_any, w_ref, gh_ref, gw_ref,
+    g, acc, rx1, rx2, up, dn, wbuf, hid_ref, zacc, zup, zdn, za, zb,
     gsend, grecv, send1, recv1, send2, recv2, usend, urecv, dsend, drecv, wsem,
     zusend, zurecv, zdsend, zdrecv, zsend1, zrecv1, zsend2, zrecv2, hsem,
 ):
@@ -77,24 +77,15 @@
             device_id=target, device_id_type=MESH,
         )
 
-    def own_rows(i):
-        return pl.ds(pl.multiple_of(i * half, half), half)
-
     def exchange(off):
         target = {"node": (node + off) % nodes}
-        return (
-            remote(st_ref, gt.at[own_rows(node)], gsend.at[0, off], grecv.at[0, off], target),
-            remote(s_ref, g.at[node], gsend.at[1, off], grecv.at[1, off], target),
-        )
+        return remote(s_ref, g.at[node], gsend.at[off], grecv.at[off], target)
 
     for off in range(1, nodes):
-        for copy in exchange(off):
-            copy.start()
-    gt[own_rows(node), :] = st_ref[...]
+        exchange(off).start()
     g[node] = s_ref[...]
     for off in range(1, nodes):
-        for copy in exchange(off):
-            copy.wait()
+        exchange(off).wait()
     fetch.wait()
 
     def first(kind, c):
@@ -123,8 +114,12 @@
         units = hid_ref[:, cols]
 
         def one(z, carry):
-            part = gt[pl.ds(pl.multiple_of(z * 4 * rows, 4 * rows), 4 * rows), :]
-            product = jnp.dot(part, units, preferred_element_type=F32).astype(BF16)
+            tall = 4 * rows
+            start = pl.multiple_of((z * tall) % half, tall)
+            part = g[(z * tall) // half, :, pl.ds(start, tall)]
+            product = lax.dot_general(
+                part, units, (((0,), (0,)), ((), ())), preferred_element_type=F32
+            ).astype(BF16)
             product = product.reshape(2, 2, rows, wide)
             into[0, c, z] = product[..., :LANES]
             into[1, c, z] = product[..., LANES:]
@@ -397,14 +392,13 @@
     grad_hidden, grad_weight = pl.pallas_call(
         functools.partial(kernel, (nodes, depth, chunks, zchunks)),
         out_shape=(
-            jax.ShapeDtypeStruct((slots, total_chunks * wide), BF16),
-            jax.ShapeDtypeStruct((rows, total_chunks * wide), BF16),
+            pltpu.VMEM((slots, total_chunks * wide), BF16),
+            pltpu.VMEM((rows, total_chunks * wide), BF16),
         ),
-        in_specs=[vmem, vmem] + [pl.BlockSpec(memory_space=pl.ANY)] * 2,
+        in_specs=[vmem] + [pl.BlockSpec(memory_space=pl.ANY)] * 2,
         out_specs=(vmem, vmem),
         scratch_shapes=[
             pltpu.VMEM((nodes, slots, half), BF16),
-            pltpu.VMEM((model, slots), BF16),
             pltpu.VMEM((2, chunks, depth, 2, 2, rows, LANES), BF16),
             pltpu.VMEM((2, chunks, depth, 2, rows, LANES), BF16),
             pltpu.VMEM((2, chunks, depth, rows, LANES), BF16),
@@ -417,8 +411,8 @@
             pltpu.VMEM((zchunks, depth, 2, 2, 2, rows, LANES), BF16),
             pltpu.VMEM((2, zchunks, 2, rows, LANES), BF16),
             pltpu.VMEM((2, zchunks, rows, LANES), BF16),
-            dma((2, nodes)),
-            dma((2, nodes)),
+            dma((nodes,)),
+            dma((nodes,)),
             dma((2, chunks)),
             dma((2, chunks)),
             dma((2, chunks)),
@@ -439,9 +433,9 @@
             dma(()),
         ],
         compiler_params=pltpu.CompilerParams(
-            collective_id=0, has_side_effects=True, vmem_limit_bytes=60 * 1024 * 1024
+            collective_id=0, has_side_effects=True, vmem_limit_bytes=54 * 1024 * 1024
         ),
-    )(scaled, scaled.T, hidden, w_down)
+    )(scaled, hidden, w_down)
     return grad_hidden[:, :units], grad_weight[:, :units]
 
 

time: 141 us -> 131 us (0.929)
  Pallas kernels: 131 us -> 125 us
  local copies, waits for them, and re-layouts: 7.16 us -> 2.46 us
    pallas_call x1, Pallas kernels: 131 us -> 125 us  [body(): pl.pallas_call(functools.partial(kernel, (nodes, depth, chunks, zchunks))...]
    unnamed x7 -> x2, local copies, waits for them, and re-layouts: 5.99 us -> 2.46 us
    select_n x1, other arithmetic: 0.2 us -> 2.27 us  [body(): scaled = jnp.where(live[:, None], scaled, jnp.zeros_like(scaled))]
where the time goes in v4:
time: 131 us
  Pallas kernels  125 us (95%)
  local copies, waits for them, and re-layouts  2.46 us (2%)
  other arithmetic  2.27 us (2%)
    pallas_call x1, Pallas kernels, body(): pl.pallas_call(functools.partial(kernel, (nodes, depth, chunks, zchunks))...  125 us

profile of v4, /device:TPU:0, one launch (start us, length us, event | category | flops | bytes accessed | tf_op | source)
XLA Modules:
  0.0 130.6 jit_solution(14720409145558489973)
XLA Ops:
  1.3 2.3 %fusion.s_ref = bf16[384,1024]{1,0:T(8,128)(2,1)} fusion(bf16[384,1024]{1,0:T(8,128)(2,1)} %param.5, f32[384]{0:T(512)} %param.6, pred[384]{0:T(512)(128)(4,1)S(1)} %iota_compare_fusion), kind=kLoop, calls=%fused_computation.1 | loop fusion | flops 1572864 | bytes 1574784 | tf_op jit(solution)/shard_map/jit(_where)/select_n | solution.py:386
  3.6 124.5 %shard_map.68 = (bf16[384,3584]{1,0:T(8,128)(2,1)S(1)}, bf16[128,3584]{1,0:T(8,128)(2,1)S(1)}) custom-call(bf16[384,1024]{1,0:T(8,128)(2,1)} %fusion.s_ref, bf16[384,3584]{1,0:T(8,128)(2,1)} %hid_any.1, bf16[2048,3584]{1,0:T(8,128)(2,1)} %w_ref.1), custom_call_target="tpu_custom_call" | custom-call | tf_op jit(solution)/shard_map/pallas_call | solution.py:392
  128.1 1.5 %copy.9 = bf16[384,3584]{1,0:T(8,128)(2,1)} copy(bf16[384,3584]{1,0:T(8,128)(2,1)S(1)} %get-tuple-element.2) | data formatting | bytes 5505024
  129.6 0.9 copy.10
  (1 shorter events, 0.0 us)
